TPU v7x, 32 devices: a whole 2x2x4 slice. The times are simulated.
32 devices in a mesh: seq: 4 (over z), fsdp: 8 (over y, x, core).
Axes of the slice: x: 2, y: 2, z: 4, core: 2. Of those that a mesh axis runs over, the one named last changes fastest.
Arguments:
- tokens: bfloat16 [8, 1024, 2048], P('fsdp', 'seq'), may hold values from -6 to 6
- cotangent: bfloat16 [8, 1024, 2048], P('fsdp', 'seq'), may hold values from -6 to 6
- lengths: int32 [8], P('fsdp'), may hold values from 256 to 1024, as said below
- routes: int32 [8, 1024, 8], P('fsdp', 'seq'), may hold values from 0 to 31, as said below
- slots: int32 [8, 1024, 8], P('fsdp', 'seq'), may hold values from -1 to 79, as said below
- w_qkv: bfloat16 [2048, 5120], P(('seq', 'fsdp')), may hold values from -0.125 to 0.125
- w_out: bfloat16 [4096, 2048], P(('seq', 'fsdp')), may hold values from -1.5 to 1.5
- w_router: bfloat16 [2048, 32], P(('seq', 'fsdp')), may hold values from -0.25 to 0.25
- norm_gains: bfloat16 [4352], P(('seq', 'fsdp')), may hold values from 0.25 to 1.75
- w_gate_up: bfloat16 [32, 2048, 1536], P('fsdp', 'seq'), may hold values from -0.125 to 0.125
- w_down: bfloat16 [32, 768, 2048], P('fsdp', None, 'seq'), may hold values from -0.625 to 0.625
Outputs:
- output: bfloat16 [8, 1024, 2048], P('fsdp', 'seq')
- d_input: float32 [8, 1024, 2048], P('fsdp', 'seq')
- grad_qkv: float32 [2048, 5120], P(('seq', 'fsdp'))
- grad_out: float32 [4096, 2048], P(('seq', 'fsdp'))
- grad_router: float32 [2048, 32], P(('seq', 'fsdp'))
- grad_gains: float32 [4352], P(('seq', 'fsdp'))
- grad_gate_up: float32 [32, 2048, 1536], P('fsdp', 'seq')
- grad_down: float32 [32, 768, 2048], P('fsdp', None, 'seq')
Inputs may be any that keep to these rules, and one draw needn't show every extreme that they name: `lengths`: every length is at least a quarter of 1024, and some sequence is 1024 long. `routes`: each token names 8 different experts. Among the valid tokens of one device (aligned blocks of 256 positions of a sequence) that route to one expert, the slots count 0, 1, 2 and so on in order of position while below 80; later ones and all padded slots are -1. In every draw some device sends 80 rows to some expert.
All inputs are finite; a program needn't handle non-finite values.
Results may differ from a plain program's by a relative error of at most 0.019.
Values may be sent and summed in bfloat16 or wider, within the bound.
A program may use at most 384 MiB of HBM per device.

v0:
```python
import jax
import jax.numpy as jnp
from jax import lax
from jax.sharding import PartitionSpec as P

QH = 32
KH = 4
HD = 128
FF = 768
TOPK = 8
EPSILON = 1e-06
THETA = 1000000.0
MASKED = -1e30


def rms_forward(values, gain):
    factor = lax.rsqrt(jnp.mean(values * values, axis=-1, keepdims=True) + EPSILON)
    return (values * factor * gain, factor)


def rms_backward(values, factor, gain, upstream):
    normed = values * factor
    scaled = upstream * gain
    inner = jnp.mean(scaled * normed, axis=-1, keepdims=True)
    grad_values = factor * (scaled - normed * inner)
    grad_gain = jnp.sum((upstream * normed).reshape(-1, values.shape[-1]), axis=0)
    return (grad_values, grad_gain)


def rotate(values, cosine, sine):
    half_dim = values.shape[-1] // 2
    first_half = values[..., :half_dim]
    second_half = values[..., half_dim:]
    return jnp.concatenate(
        [first_half * cosine - second_half * sine, second_half * cosine + first_half * sine],
        axis=-1,
    )


def to_experts(rows, groups):
    shaped = rows.reshape(groups, -1, rows.shape[-1])
    return lax.all_to_all(shaped, "fsdp", split_axis=0, concat_axis=0, tiled=True)


def from_experts(rows):
    returned = lax.all_to_all(rows, "fsdp", split_axis=0, concat_axis=0, tiled=True)
    return returned.reshape(-1, returned.shape[-1])


def expert_weights(w_gate_up, w_down):
    return (
        lax.all_gather(w_gate_up, "seq", axis=1, tiled=True),
        lax.all_gather(w_down, "seq", axis=2, tiled=True),
    )


def per_device(
    tokens, cotangent, lengths, routes, slots, w_qkv, w_out, w_router, norm_gains, w_gate_up, w_down
):
    tok_count = tokens.shape[1]
    width = tokens.shape[2]
    seq_parts = lax.axis_size("seq")
    fsdp_parts = lax.axis_size("fsdp")
    local_experts = w_gate_up.shape[0]
    heads_local = QH // seq_parts
    kv_local = KH // seq_parts
    group_size = QH // KH
    seq_total = tok_count * seq_parts
    layer_inputs = tokens[0].astype(jnp.float32)
    full_qkv, full_out, full_router, full_gains = (
        lax.all_gather(w_qkv, ("seq", "fsdp"), axis=0, tiled=True),
        lax.all_gather(w_out, ("seq", "fsdp"), axis=0, tiled=True),
        lax.all_gather(w_router, ("seq", "fsdp"), axis=0, tiled=True),
        lax.all_gather(norm_gains, ("seq", "fsdp"), axis=0, tiled=True),
    )
    gain_values = full_gains.astype(jnp.float32)
    gain_attn = gain_values[:width]
    gain_ffn = gain_values[width : 2 * width]
    gain_query = gain_values[2 * width : 2 * width + HD]
    gain_key = gain_values[2 * width + HD :]
    expert_count = full_router.shape[1]
    capacity = tok_count * TOPK * 5 // (4 * expert_count)
    total_slots = expert_count * capacity
    attn_normed, attn_factor = rms_forward(layer_inputs, gain_attn)
    attention_reduced = attn_normed.astype(jnp.bfloat16)
    projected_rows = jnp.dot(attention_reduced, full_qkv, preferred_element_type=jnp.float32)
    query_raw = projected_rows[:, : QH * HD].reshape(tok_count, QH, HD)
    key_raw = projected_rows[:, QH * HD : (QH + KH) * HD].reshape(tok_count, KH, HD)
    value_raw = projected_rows[:, (QH + KH) * HD :].reshape(tok_count, KH, HD)
    query_normed, query_factor = rms_forward(query_raw, gain_query)
    key_normed, key_factor = rms_forward(key_raw, gain_key)
    positions = lax.axis_index("seq") * tok_count + jnp.arange(tok_count, dtype=jnp.int32)
    frequency = THETA ** (-jnp.arange(HD // 2, dtype=jnp.float32) / (HD // 2))
    angles = positions.astype(jnp.float32)[:, None] * frequency[None, :]
    cosine = jnp.cos(angles)[:, None, :]
    sine = jnp.sin(angles)[:, None, :]
    query_send = (
        rotate(query_normed, cosine, sine)
        .astype(jnp.bfloat16)
        .reshape(tok_count, seq_parts, heads_local, HD)
    )
    kv_stack = jnp.stack([rotate(key_normed, cosine, sine), value_raw], axis=2)
    kv_send = kv_stack.astype(jnp.bfloat16)
    query_heads, kv_heads = (
        lax.all_to_all(query_send, "seq", split_axis=1, concat_axis=0, tiled=True),
        lax.all_to_all(kv_send, "seq", split_axis=1, concat_axis=0, tiled=True),
    )
    key_all = kv_heads[:, :, 0]
    value_all = kv_heads[:, :, 1]
    seq_length = lengths[0]
    block = min(512, seq_total)
    block_count = seq_total // block
    scale = HD ** (-0.5)
    query_blocks = query_heads.reshape(block_count, block, kv_local, group_size, HD)
    starts = jnp.arange(block_count, dtype=jnp.int32) * block
    key_index = jnp.arange(seq_total, dtype=jnp.int32)

    def block_scores(start, query_block):
        scores = (
            jnp.einsum("qkgd,pkd->kgqp", query_block, key_all, preferred_element_type=jnp.float32)
            * scale
        )
        query_index = start + jnp.arange(block, dtype=jnp.int32)
        allowed = (key_index[None, :] <= query_index[:, None]) & (key_index[None, :] < seq_length)
        return jnp.where(allowed, scores, MASKED)

    def attend_block(pieces):
        start, query_block = pieces
        scores = block_scores(start, query_block)
        peak = jnp.max(scores, axis=-1, keepdims=True)
        weights = jnp.exp(scores - peak)
        totals = jnp.sum(weights, axis=-1, keepdims=True)
        probs = weights / totals
        mixed_tokens = jnp.einsum(
            "kgqp,pkd->qkgd",
            probs.astype(jnp.bfloat16),
            value_all,
            preferred_element_type=jnp.float32,
        )
        return (mixed_tokens.astype(jnp.bfloat16), (peak + jnp.log(totals))[..., 0])

    attn_blocks, log_totals = lax.map(attend_block, (starts, query_blocks))
    attn_send = attn_blocks.reshape(seq_total, 1, heads_local, HD)
    attn_tokens = lax.all_to_all(attn_send, "seq", split_axis=0, concat_axis=1, tiled=True).reshape(
        tok_count, QH * HD
    )
    residual_stream = layer_inputs + jnp.dot(
        attn_tokens, full_out, preferred_element_type=jnp.float32
    )
    ffn_normed, ffn_factor = rms_forward(residual_stream, gain_ffn)
    feedforward_reduced = ffn_normed.astype(jnp.bfloat16)
    router_scores = jnp.dot(feedforward_reduced, full_router, preferred_element_type=jnp.float32)
    route_rows = routes[0]
    slot_rows = slots[0]
    picked = route_rows[:, :, None] == jnp.arange(expert_count, dtype=jnp.int32)[None, None, :]
    selected = jnp.sum(jnp.where(picked, router_scores[:, None, :], 0.0), axis=-1)
    gate_prob = jax.nn.softmax(selected, axis=-1)
    flat_pos = jnp.where(slot_rows >= 0, route_rows * capacity + slot_rows, total_slots).reshape(-1)
    owner = (
        jnp.full((total_slots,), tok_count * TOPK, jnp.int32)
        .at[flat_pos]
        .set(jnp.arange(tok_count * TOPK, dtype=jnp.int32), mode="drop")
    )
    send_rows = jnp.take(feedforward_reduced, owner // TOPK, axis=0, mode="fill", fill_value=0)
    received = to_experts(send_rows, fsdp_parts)
    expert_rows = received.reshape(fsdp_parts, local_experts, capacity, width)
    full_gate_up, full_down = expert_weights(w_gate_up, w_down)
    gate_up = jnp.einsum(
        "sjcd,jdf->sjcf", expert_rows, full_gate_up, preferred_element_type=jnp.float32
    )
    gate_part = gate_up[..., :FF]
    up_part = gate_up[..., FF:]
    hidden_low = (jax.nn.silu(gate_part) * up_part).astype(jnp.bfloat16)
    expert_out = jnp.einsum(
        "sjch,jhd->sjcd", hidden_low, full_down, preferred_element_type=jnp.float32
    ).astype(jnp.bfloat16)
    returned = from_experts(expert_out.reshape(fsdp_parts, local_experts * capacity, width))
    token_out = jnp.take(returned, flat_pos, axis=0, mode="fill", fill_value=0).reshape(
        tok_count, TOPK, width
    )
    token_wide = token_out.astype(jnp.float32)
    moe_out = jnp.sum(gate_prob[:, :, None] * token_wide, axis=1)
    valid = positions < seq_length
    final = jnp.where(valid[:, None], residual_stream + moe_out, 0.0)
    grad_final = jnp.where(valid[:, None], cotangent[0].astype(jnp.float32), 0.0)
    grad_prob = jnp.sum(token_wide * grad_final[:, None, :], axis=-1)
    grad_selected = gate_prob * (grad_prob - jnp.sum(gate_prob * grad_prob, axis=-1, keepdims=True))
    grad_logits = jnp.sum(jnp.where(picked, grad_selected[:, :, None], 0.0), axis=1).astype(
        jnp.bfloat16
    )
    grad_token_out = (
        (gate_prob[:, :, None] * grad_final[:, None, :])
        .astype(jnp.bfloat16)
        .reshape(tok_count * TOPK, width)
    )
    grad_send = jnp.take(grad_token_out, owner, axis=0, mode="fill", fill_value=0)
    grad_rows = to_experts(grad_send, fsdp_parts).reshape(
        fsdp_parts, local_experts, capacity, width
    )
    again_gate_up, again_down = expert_weights(w_gate_up, w_down)
    grad_hidden_low = jnp.einsum(
        "sjcd,jhd->sjch", grad_rows, again_down, preferred_element_type=jnp.float32
    ).astype(jnp.bfloat16)
    grad_hidden = lax.optimization_barrier(grad_hidden_low).astype(jnp.float32)
    sigmoid_gate = jax.nn.sigmoid(gate_part)
    grad_gate = grad_hidden * up_part * sigmoid_gate * (1.0 + gate_part * (1.0 - sigmoid_gate))
    grad_up = grad_hidden * gate_part * sigmoid_gate
    grad_gu_low = jnp.concatenate([grad_gate, grad_up], axis=-1).astype(jnp.bfloat16)
    grad_expert_rows = jnp.einsum(
        "sjcf,jdf->sjcd", grad_gu_low, again_gate_up, preferred_element_type=jnp.float32
    ).astype(jnp.bfloat16)
    grad_back = from_experts(grad_expert_rows.reshape(fsdp_parts, local_experts * capacity, width))
    partial_gate_up = jnp.einsum(
        "sjcd,sjcf->jdf", expert_rows, grad_gu_low, preferred_element_type=jnp.float32
    )
    partial_down = jnp.einsum(
        "sjch,sjcd->jhd", hidden_low, grad_rows, preferred_element_type=jnp.float32
    )
    grad_gate_up, grad_down = (
        lax.psum_scatter(
            partial_gate_up.astype(jnp.bfloat16), "seq", scatter_dimension=1, tiled=True
        ).astype(jnp.float32),
        lax.psum_scatter(
            partial_down.astype(jnp.bfloat16), "seq", scatter_dimension=2, tiled=True
        ).astype(jnp.float32),
    )
    grad_from_rows = jnp.sum(
        jnp.take(grad_back, flat_pos, axis=0, mode="fill", fill_value=0)
        .reshape(tok_count, TOPK, width)
        .astype(jnp.float32),
        axis=1,
    )
    grad_ffn = grad_from_rows + jnp.einsum(
        "te,de->td", grad_logits, full_router, preferred_element_type=jnp.float32
    )
    grad_router_local = jnp.einsum(
        "td,te->de", feedforward_reduced, grad_logits, preferred_element_type=jnp.float32
    )
    grad_res_norm, grad_gain_ffn = rms_backward(residual_stream, ffn_factor, gain_ffn, grad_ffn)
    grad_residual = grad_final + grad_res_norm
    grad_attn_low = grad_residual.astype(jnp.bfloat16)
    grad_out_local = jnp.einsum(
        "te,td->ed", attn_tokens, grad_attn_low, preferred_element_type=jnp.float32
    )
    grad_attn_tokens = jnp.einsum(
        "td,ed->te", grad_attn_low, full_out, preferred_element_type=jnp.float32
    ).astype(jnp.bfloat16)
    grad_heads_send = grad_attn_tokens.reshape(tok_count, seq_parts, heads_local, HD)
    grad_attn_heads = lax.all_to_all(
        grad_heads_send, "seq", split_axis=1, concat_axis=0, tiled=True
    ).reshape(block_count, block, kv_local, group_size, HD)

    def attend_back(carry, pieces):
        start, query_block, grad_block, log_block = pieces
        scores = block_scores(start, query_block)
        probs = jnp.exp(scores - log_block[..., None])
        grad_probs = jnp.einsum(
            "qkgd,pkd->kgqp", grad_block, value_all, preferred_element_type=jnp.float32
        )
        inner = jnp.sum(probs * grad_probs, axis=-1, keepdims=True)
        grad_scores = (probs * (grad_probs - inner)).astype(jnp.bfloat16)
        grad_query = (
            jnp.einsum("kgqp,pkd->qkgd", grad_scores, key_all, preferred_element_type=jnp.float32)
            * scale
        )
        grad_key = (
            carry[0]
            + jnp.einsum(
                "kgqp,qkgd->pkd", grad_scores, query_block, preferred_element_type=jnp.float32
            )
            * scale
        )
        grad_value = carry[1] + jnp.einsum(
            "kgqp,qkgd->pkd",
            probs.astype(jnp.bfloat16),
            grad_block,
            preferred_element_type=jnp.float32,
        )
        return ((grad_key, grad_value), grad_query.astype(jnp.bfloat16))

    zeros_kv = jnp.zeros((seq_total, kv_local, HD), jnp.float32)
    kv_grads, grad_query_blocks = lax.scan(
        attend_back, (zeros_kv, zeros_kv), (starts, query_blocks, grad_attn_heads, log_totals)
    )
    grad_query_send = grad_query_blocks.reshape(seq_total, 1, heads_local, HD)
    grad_kv_send = jnp.stack([kv_grads[0], kv_grads[1]], axis=2).astype(jnp.bfloat16)
    grad_query_tok, grad_kv_tok = (
        lax.all_to_all(grad_query_send, "seq", split_axis=0, concat_axis=1, tiled=True),
        lax.all_to_all(grad_kv_send, "seq", split_axis=0, concat_axis=1, tiled=True),
    )
    grad_query_rot = grad_query_tok.reshape(tok_count, QH, HD).astype(jnp.float32)
    grad_kv_pair = grad_kv_tok.astype(jnp.float32)
    grad_query_norm = rotate(grad_query_rot, cosine, -sine)
    grad_key_norm = rotate(grad_kv_pair[:, :, 0], cosine, -sine)
    grad_query_raw, grad_gain_query = rms_backward(
        query_raw, query_factor, gain_query, grad_query_norm
    )
    grad_key_raw, grad_gain_key = rms_backward(key_raw, key_factor, gain_key, grad_key_norm)
    grad_projected = jnp.concatenate(
        [
            grad_query_raw.reshape(tok_count, -1),
            grad_key_raw.reshape(tok_count, -1),
            grad_kv_pair[:, :, 1].reshape(tok_count, -1),
        ],
        axis=-1,
    ).astype(jnp.bfloat16)
    grad_qkv_local = jnp.einsum(
        "td,te->de", attention_reduced, grad_projected, preferred_element_type=jnp.float32
    )
    grad_attn_norm = jnp.einsum(
        "te,de->td", grad_projected, full_qkv, preferred_element_type=jnp.float32
    )
    grad_in_norm, grad_gain_attn = rms_backward(
        layer_inputs, attn_factor, gain_attn, grad_attn_norm
    )
    grad_inputs = grad_residual + grad_in_norm
    grad_gain_local = jnp.concatenate(
        [grad_gain_attn, grad_gain_ffn, grad_gain_query, grad_gain_key]
    )
    grad_qkv, grad_out, grad_router, grad_gains = (
        lax.psum_scatter(grad_qkv_local, ("seq", "fsdp"), scatter_dimension=0, tiled=True),
        lax.psum_scatter(grad_out_local, ("seq", "fsdp"), scatter_dimension=0, tiled=True),
        lax.psum_scatter(grad_router_local, ("seq", "fsdp"), scatter_dimension=0, tiled=True),
        lax.psum_scatter(grad_gain_local, ("seq", "fsdp"), scatter_dimension=0, tiled=True),
    )
    return (
        final.astype(jnp.bfloat16)[None],
        grad_inputs[None],
        grad_qkv,
        grad_out,
        grad_router,
        grad_gains,
        grad_gate_up,
        grad_down,
    )


def solution(mesh):
    in_specs = (
        P("fsdp", "seq", None),
        P("fsdp", "seq", None),
        P("fsdp"),
        P("fsdp", "seq", None),
        P("fsdp", "seq", None),
        P(("seq", "fsdp"), None),
        P(("seq", "fsdp"), None),
        P(("seq", "fsdp"), None),
        P(("seq", "fsdp")),
        P("fsdp", "seq", None),
        P("fsdp", None, "seq"),
    )
    out_specs = (
        P("fsdp", "seq", None),
        P("fsdp", "seq", None),
        P(("seq", "fsdp"), None),
        P(("seq", "fsdp"), None),
        P(("seq", "fsdp"), None),
        P(("seq", "fsdp")),
        P("fsdp", "seq", None),
        P("fsdp", None, "seq"),
    )
    return jax.shard_map(
        per_device, mesh=mesh, in_specs=in_specs, out_specs=out_specs, check_vma=False
    )
```

profile of v0, /device:TPU:1, one launch (start us, length us, event | category | flops | bytes accessed | tf_op | source)
XLA Modules:
  0.0 2935.8 jit_solution(3015769868315914340)
XLA Ops:
  10.8 43.2 %all-reduce = bf16[4352]{0:T(1024)(128)(2,1)S(1)} all-reduce(bf16[4352]{0:T(1024)(128)(2,1)S(1)} %dynamic-update-slice), channel_id=1, replica_groups=mesh['seq'=4,'fsdp'=8] {'seq','fsdp'}, use_global_device_ids=true, to_apply=%add | all-reduce | flops 4352 | bytes 17408
  55.0 93.7 %all-gather.6.cloned.1.call-done = bf16[2048,5120]{1,0:T(8,128)(2,1)} async-done(((bf16[64,5120]{1,0:T(8,128)(2,1)}), bf16[2048,5120]{1,0:T(8,128)(2,1)}) %all-gather.6.cloned.1.call-update) | async-done | bytes 20971536 | tf_op jit(solution)/shard_map/all_gather | solution.py:71
  193.0 87.5 %all-to-all-done = bf16[256,4,8,128]{0,3,2,1:T(8,128)(2,1)S(1)} async-done(((bf16[256,4,8,128]{0,3,2,1:T(8,128)(2,1)}), bf16[256,4,8,128]{0,3,2,1:T(8,128)(2,1)S(1)}, u32[]{:S(2)}, u32[]{:S(2)}) %all-to-all-start) | async-done | bytes 2097184 | tf_op jit(solution)/shard_map/all_to_all | solution.py:105
  286.6 33.9 %while.30 = (s32[]{:T(128)}, bf16[2,512,1,8,128]{4,3,1,0,2:T(8,128)(2,1)}, f32[2,1,8,512]{3,2,1,0:T(8,128)S(1)}, s32[2]{0:T(128)S(1)}, s32[]{:T(128)}, /*index=5...) while((s32[]{:T(128)}, ...), condition=%wide.region_6.7_spmd.clone.clone, body=%wide.region_3.6_spmd.clone.clone.sunk | while | flops 2199385600 | bytes 57285240 | solution.py:142
  339.3 99.5 %all-to-all-done.2 = bf16[1024,1,8,128]{3,2,1,0:T(8,128)(2,1)} async-done(((bf16[1024,1,8,128]{3,2,1,0:T(8,128)(2,1)}), bf16[1024,1,8,128]{3,2,1,0:T(8,128)(2,1)}, u32[]{:S(2)}, u32[]{:S(2)}) %all-to-all-start.2) | async-done | bytes 2097184 | tf_op jit(solution)/shard_map/all_to_all | solution.py:144
  480.3 290.4 %all-gather.10.cloned.1.call-done = bf16[4,2048,1536]{2,1,0:T(8,128)(2,1)} async-done(((bf16[4,512,1536]{2,1,0:T(8,128)(2,1)}), bf16[4,2048,1536]{2,1,0:T(8,128)(2,1)}) %all-gather.10.cloned.1.call-update) | async-done | bytes 25165840 | tf_op jit(solution)/shard_map/all_gather | solution.py:52
  770.7 25.7 fusion.75
  804.5 183.9 %all-gather.12.cloned.1.call-done = bf16[4,768,2048]{2,1,0:T(8,128)(2,1)} async-done(((bf16[4,768,512]{2,1,0:T(8,128)(2,1)}), bf16[4,768,2048]{2,1,0:T(8,128)(2,1)}) %all-gather.12.cloned.1.call-update) | async-done | bytes 12582928 | tf_op jit(solution)/shard_map/all_gather | solution.py:53
  988.5 16.0 convert_bitcast_fusion.2
  1021.0 145.7 %all-gather = bf16[32,64,32]{1,2,0:T(8,128)(2,1)S(1)} all-gather(bf16[1,64,32]{1,2,0:T(8,128)(2,1)S(1)} %bitcast.454), channel_id=1, replica_groups=mesh['seq'=4,'fsdp'=8] {'seq','fsdp'}, dimensions={0}, use_global_device_ids=true | all-gather | bytes 135168 | tf_op jit(solution)/shard_map/all_gather | solution.py:73
  1169.3 21.6 gather_fusion.2
  1201.4 24.6 gather_fusion.1
  1243.5 121.0 %all-to-all-done.5 = bf16[8,320,2048]{2,1,0:T(8,128)(2,1)} async-done(((bf16[8,320,2048]{2,1,0:T(8,128)(2,1)}), bf16[8,320,2048]{2,1,0:T(8,128)(2,1)}, u32[]{:S(2)}, u32[]{:S(2)}) %all-to-all-start.5) | async-done | bytes 10485792 | tf_op jit(solution)/shard_map/all_to_all | solution.py:42
  1364.5 16.6 bitcast_convert_fusion.1
  1381.7 16.3 convert_bitcast_fusion.4
  1408.6 27.0 bitcast_convert_fusion
  1435.8 23.5 convert_bitcast_fusion.1
  1469.4 125.6 %all_to_all.101 = bf16[8,320,2048]{2,1,0:T(8,128)(2,1)} all-to-all(bf16[8,320,2048]{2,1,0:T(8,128)(2,1)} %bitcast.424), channel_id=1, replica_groups=mesh['seq'=4,'fsdp'=8] {'fsdp'}, dimensions={0} | all-to-all | bytes 20971520 | tf_op jit(solution)/shard_map/all_to_all | solution.py:46
  1595.0 21.7 gather_fusion.3
  1616.7 17.4 convert_reduce_fusion
  1637.6 13.2 fusion.114
  1650.8 18.6 fusion.106
  1677.0 104.5 %all-to-all-done.7 = bf16[256,4,8,128]{3,2,0,1:T(8,128)(2,1)S(1)} async-done(((bf16[256,4,8,128]{3,2,0,1:T(8,128)(2,1)}), bf16[256,4,8,128]{3,2,0,1:T(8,128)(2,1)S(1)}, u32[]{:S(2)}, u32[]{:S(2)}) %all-to-all-start.7) | async-done | bytes 2097184 | tf_op jit(solution)/shard_map/all_to_all | solution.py:249
  1783.1 91.1 %while.31 = (s32[]{:T(128)}, f32[1024,1,128]{0,2,1:T(8,128)}, f32[1024,1,128]{0,2,1:T(8,128)}, bf16[2,512,1,8,128]{4,3,1,0,2:T(8,128)(2,1)}, bf16[2,512,1,8,128]...) while((s32[]{:T(128)}, f32[1024,1,128]{0,2,1:T(8,128)}, ...), condition=%wide.region_20.22_spmd.clone.clone, body=%wide.region_18.21_spmd.clone.clone.sunk | while | flops 5409207808 | bytes 199187792 | solution.py:282
  1837.2 11.1 fusion.196
  1877.3 30.9 %all_to_all.102 = bf16[1024,1,2,128]{3,2,1,0:T(2,128)(2,1)S(1)} all-to-all(bf16[1024,1,2,128]{3,2,1,0:T(2,128)(2,1)S(1)} %copy.408), channel_id=1, replica_groups=mesh['seq'=4,'fsdp'=8] {'seq'}, dimensions={0} | all-to-all | bytes 1048576 | tf_op jit(solution)/shard_map/all_to_all | solution.py:289
  1925.4 86.4 %all-to-all-done.8 = bf16[1024,1,8,128]{3,2,1,0:T(8,128)(2,1)S(1)} async-done(((bf16[1024,1,8,128]{3,2,1,0:T(8,128)(2,1)}), bf16[1024,1,8,128]{3,2,1,0:T(8,128)(2,1)S(1)}, u32[]{:S(2)}, u32[]{:S(2)}) %all-to-all-start.8) | async-done | bytes 2097184 | tf_op jit(solution)/shard_map/all_to_all | solution.py:288
  2049.5 18.2 fusion.107
  2099.0 12.0 fusion.104
  2111.1 66.4 %all-reduce.1 = f32[4352]{0:T(1024)S(1)} all-reduce(f32[4352]{0:T(1024)S(1)} %pad_maximum_fusion.9), channel_id=5, replica_groups=mesh['seq'=4,'fsdp'=8] {'seq','fsdp'}, use_global_device_ids=true, to_apply=%region_31.33.clone | all-reduce | flops 4352 | bytes 34816
  2196.6 278.3 %reduce-scatter.10.cloned.1.call-done = f32[128,2048]{1,0:T(8,128)} async-done(((f32[4096,2048]{1,0:T(8,128)}), f32[128,2048]{1,0:T(8,128)}) %reduce-scatter.10.cloned.1.call-update) | async-done | bytes 1048592 | tf_op jit(solution)/shard_map/reduce_scatter | solution.py:322
  2474.9 454.0 %reduce-scatter.8.cloned.1.call-done = f32[64,5120]{1,0:T(8,128)} async-done(((f32[2048,5120]{1,0:T(8,128)}), f32[64,5120]{1,0:T(8,128)}) %reduce-scatter.8.cloned.1.call-update) | async-done | bytes 1310736 | tf_op jit(solution)/shard_map/reduce_scatter | solution.py:321
  (378 shorter events, 424.4 us)
Async XLA Ops:
  7.2 46.9 %copy-start.11 = (bf16[1,256,2048]{2,1,0:T(8,128)(2,1)S(1)}, bf16[1,256,2048]{2,1,0:T(8,128)(2,1)}, u32[]{:S(2)}) copy-start(bf16[1,256,2048]{2,1,0:T(8,128)(2,1)} %param.17) | copy-start | bytes 3145732
  7.2 141.6 %all-gather.6.cloned.1.call-start = ((), (), s32[]{:S(2)}) async-start(), calls=%async_computation.15 | async-start | bytes 21626880 | tf_op jit(solution)/shard_map/all_gather | solution.py:71
  7.9 435.2 %all-gather.8.cloned.1.call-start = ((), (), s32[]{:S(2)}) async-start(), calls=%async_computation.16 | async-start | bytes 17301504 | tf_op jit(solution)/shard_map/all_gather | solution.py:72
  8.7 762.0 %all-gather.10.cloned.1.call-start = ((), (), s32[]{:S(2)}) async-start(), calls=%async_computation.17 | async-start | bytes 31457280 | tf_op jit(solution)/shard_map/all_gather | solution.py:52
  10.4 175.6 %copy-start.32 = (f32[256,64]{0,1:T(8,128)}, f32[256,64]{0,1:T(8,128)S(1)}, u32[]{:S(2)}) copy-start(f32[256,64]{0,1:T(8,128)S(1)} %get-tuple-element.494) | copy-start | bytes 196612
  10.5 151.7 %copy-start.28 = (f32[256,64]{1,0:T(8,128)}, f32[256,64]{1,0:T(8,128)S(1)}, u32[]{:S(2)}) copy-start(f32[256,64]{1,0:T(8,128)S(1)} %copy.374) | copy-start | bytes 196612
  54.4 94.4 %copy-start.55 = (f32[256]{0:T(256)}, f32[256]{0:T(256)S(1)}, u32[]{:S(2)}) copy-start(f32[256]{0:T(256)S(1)} %add_rsqrt_fusion.3) | copy-start | bytes 3076
  54.4 107.6 %copy-start.65 = (f32[128]{0:T(128)}, f32[128]{0:T(128)S(1)}, u32[]{:S(2)}) copy-start(f32[128]{0:T(128)S(1)} %get-tuple-element.490) | copy-start | bytes 1540
  54.4 128.6 %copy-start.63 = (f32[128]{0:T(128)}, f32[128]{0:T(128)S(1)}, u32[]{:S(2)}) copy-start(f32[128]{0:T(128)S(1)} %get-tuple-element.491) | copy-start | bytes 1540
  55.0 93.7 %copy-start.39 = (f32[2048]{0:T(1024)}, f32[2048]{0:T(1024)S(1)}, u32[]{:S(2)}) copy-start(f32[2048]{0:T(1024)S(1)} %get-tuple-element.489) | copy-start | bytes 24580
  163.4 24.7 all-to-all-start.1
  188.1 92.4 %all-to-all-start = ((bf16[256,4,8,128]{0,3,2,1:T(8,128)(2,1)}), bf16[256,4,8,128]{0,3,2,1:T(8,128)(2,1)S(1)}, u32[]{:S(2)}, u32[]{:S(2)}) async-start(bf16[256,4,8,128]{0,3,2,1:T(8,128)(2,1)} %pad_maximum_fusion.3), calls=%async_computation | async-start | bytes 4194304 | tf_op jit(solution)/shard_map/all_to_all | solution.py:105
  320.5 122.6 %copy-start.1 = (bf16[2,512,1,8,128]{4,1,3,2,0:T(8,128)(2,1)}, bf16[2,512,1,8,128]{4,1,3,2,0:T(8,128)(2,1)S(1)}, u32[]{:S(2)}) copy-start(bf16[2,512,1,8,128]{4,1,3,2,0:T(8,128)(2,1)S(1)} %get-tuple-element.702) | copy-start | bytes 6291460
  320.5 122.6 %copy-start.6 = (bf16[1024,1,128]{2,0,1:T(8,128)(2,1)}, bf16[1024,1,128]{2,0,1:T(8,128)(2,1)S(1)}, u32[]{:S(2)}) copy-start(bf16[1024,1,128]{2,0,1:T(8,128)(2,1)S(1)} %get-tuple-element.709) | copy-start | bytes 786436
  321.2 117.6 %all-to-all-start.2 = ((bf16[1024,1,8,128]{3,2,1,0:T(8,128)(2,1)}), bf16[1024,1,8,128]{3,2,1,0:T(8,128)(2,1)}, u32[]{:S(2)}, u32[]{:S(2)}) async-start(bf16[1024,1,8,128]{3,2,1,0:T(8,128)(2,1)} %bitcast.17), calls=%async_computation.2 | async-start | bytes 4194304 | tf_op jit(solution)/shard_map/all_to_all | solution.py:144
  325.7 117.4 %copy-start.12 = (bf16[1,256,2048]{2,1,0:T(8,128)(2,1)S(1)}, bf16[1,256,2048]{2,1,0:T(8,128)(2,1)}, u32[]{:S(2)}) copy-start(bf16[1,256,2048]{2,1,0:T(8,128)(2,1)} %param.17) | copy-start | bytes 3145732
  325.7 662.8 %all-gather.12.cloned.1.call-start = ((), (), s32[]{:S(2)}) async-start(), calls=%async_computation.18 | async-start | bytes 15728640 | tf_op jit(solution)/shard_map/all_gather | solution.py:53
  474.4 296.4 %all-to-all-start.3 = ((bf16[8,320,2048]{2,1,0:T(8,128)(2,1)}), bf16[8,320,2048]{2,1,0:T(8,128)(2,1)}, u32[]{:S(2)}, u32[]{:S(2)}) async-start(bf16[8,320,2048]{2,1,0:T(8,128)(2,1)} %broadcast_select_fusion.1), calls=%async_computation.3 | async-start | bytes 20971520 | tf_op jit(solution)/shard_map/all_to_all | solution.py:42
  1014.6 154.7 %all-to-all-start.4 = ((bf16[8,320,2048]{2,1,0:T(8,128)(2,1)}), bf16[8,320,2048]{2,1,0:T(8,128)(2,1)}, u32[]{:S(2)}, u32[]{:S(2)}) async-start(bf16[8,320,2048]{2,1,0:T(8,128)(2,1)} %bitcast.421), calls=%async_computation.4 | async-start | bytes 20971520 | tf_op jit(solution)/shard_map/all_to_all | solution.py:46
  1020.2 148.9 %copy-start.50 = (s32[1,256,8]{1,2,0:T(8,128)S(1)}, s32[1,256,8]{1,2,0:T(8,128)}, u32[]{:S(2)}) copy-start(s32[1,256,8]{1,2,0:T(8,128)} %param.20) | copy-start | bytes 24580
  1236.0 128.5 %all-to-all-start.5 = ((bf16[8,320,2048]{2,1,0:T(8,128)(2,1)}), bf16[8,320,2048]{2,1,0:T(8,128)(2,1)}, u32[]{:S(2)}, u32[]{:S(2)}) async-start(bf16[8,320,2048]{2,1,0:T(8,128)(2,1)} %broadcast_select_fusion), calls=%async_computation.5 | async-start | bytes 20971520 | tf_op jit(solution)/shard_map/all_to_all | solution.py:42
  1241.2 836.0 %reduce-scatter.16.cloned.1.call-start = ((), (), s32[]{:S(2)}) async-start(), calls=%async_computation.23 | async-start | bytes 1081344
  1243.4 938.1 %reduce-scatter.14.cloned.1.call-start = ((), (), s32[]{:S(2)}) async-start(), calls=%async_computation.22 | async-start | bytes 15728640 | tf_op jit(solution)/shard_map/reduce_scatter | solution.py:223
  1381.2 805.9 %reduce-scatter.12.cloned.1.call-start = ((), (), s32[]{:S(2)}) async-start(), calls=%async_computation.21 | async-start | bytes 31457280 | tf_op jit(solution)/shard_map/reduce_scatter | solution.py:220
  1435.6 1039.3 %reduce-scatter.10.cloned.1.call-start = ((), (), s32[]{:S(2)}) async-start(), calls=%async_computation.20 | async-start | bytes 34603008 | tf_op jit(solution)/shard_map/reduce_scatter | solution.py:322
  1469.4 125.6 %copy-start.48 = (s32[2048]{0:T(1024)S(1)}, s32[2048]{0:T(1024)}, u32[]{:S(2)}) copy-start(s32[2048]{0:T(1024)} %copy-done.47) | copy-start | bytes 24580
  1673.2 109.9 %copy-start.73 = (s32[2]{0:T(128)S(1)}, s32[2]{0:T(128)}, u32[]{:S(2)}) copy-start(s32[2]{0:T(128)} %copy-done.72) | copy-start | bytes 28
  1673.2 108.3 %all-to-all-start.7 = ((bf16[256,4,8,128]{3,2,0,1:T(8,128)(2,1)}), bf16[256,4,8,128]{3,2,0,1:T(8,128)(2,1)S(1)}, u32[]{:S(2)}, u32[]{:S(2)}) async-start(bf16[256,4,8,128]{3,2,0,1:T(8,128)(2,1)} %copy.394), calls=%async_computation.7 | async-start | bytes 4194304 | tf_op jit(solution)/shard_map/all_to_all | solution.py:249
  1875.5 37.3 %copy-start.35 = (f32[256,32]{0,1:T(8,128)S(1)}, f32[256,32]{0,1:T(8,128)}, u32[]{:S(2)}) copy-start(f32[256,32]{0,1:T(8,128)} %copy-done.34) | copy-start | bytes 98308
  1908.2 103.7 %all-to-all-start.8 = ((bf16[1024,1,8,128]{3,2,1,0:T(8,128)(2,1)}), bf16[1024,1,8,128]{3,2,1,0:T(8,128)(2,1)S(1)}, u32[]{:S(2)}, u32[]{:S(2)}) async-start(bf16[1024,1,8,128]{3,2,1,0:T(8,128)(2,1)} %bitcast.52), calls=%async_computation.8 | async-start | bytes 4194304 | tf_op jit(solution)/shard_map/all_to_all | solution.py:288
  1911.8 1017.0 %reduce-scatter.8.cloned.1.call-start = ((), (), s32[]{:S(2)}) async-start(), calls=%async_computation.19 | async-start | bytes 43253760 | tf_op jit(solution)/shard_map/reduce_scatter | solution.py:321
  2099.0 79.1 %copy-start.15 = (f32[256,2048]{1,0:T(8,128)S(1)}, f32[256,2048]{1,0:T(8,128)}, u32[]{:S(2)}) copy-start(f32[256,2048]{1,0:T(8,128)} %copy-done.14) | copy-start | bytes 6291460
  (65 other events, 595.4 us)
Sparse Core Ops, SparseCore 0:
  10.9 137.8 all-gather.5
  151.6 149.6 all-gather.7
  302.9 467.8 all-gather.9
  772.1 216.3 all-gather.11
  1243.9 132.1 reduce-scatter.15
  1381.3 211.5 reduce-scatter.13
  1595.3 505.6 reduce-scatter.11
  2103.8 371.0 reduce-scatter.9
  2477.8 451.0 reduce-scatter.7
where the time goes:
time: 2950 us; the launch traced here: 2940 us
  waiting for transfers between devices  1800 us (61%)
  blocking collectives  412 us (14%)
  matrix products  288 us (10%)
  local copies, waits for them, and re-layouts  220 us (7%)
  other arithmetic  159 us (5%)
  starting transfers between devices  37.8 us (1%)
    reduce_scatter x1, waiting for transfers between devices, per_device(): lax.psum_scatter(grad_qkv_local, ('seq', 'fsdp'), scatter_dimension=0, ti...  454 us
    all_gather x1, waiting for transfers between devices, expert_weights(): lax.all_gather(w_gate_up, 'seq', axis=1, tiled=True)  290 us
    reduce_scatter x1, waiting for transfers between devices, per_device(): lax.psum_scatter(grad_out_local, ('seq', 'fsdp'), scatter_dimension=0, ti...  278 us
    all_gather x1, waiting for transfers between devices, expert_weights(): lax.all_gather(w_down, 'seq', axis=2, tiled=True)  184 us
    all_gather x1, blocking collectives, per_device(): lax.all_gather(w_router, ('seq', 'fsdp'), axis=0, tiled=True)  146 us
    all_to_all x1, blocking collectives, from_experts(): lax.all_to_all(rows, 'fsdp', split_axis=0, concat_axis=0, tiled=True)  126 us
    all_to_all x2, waiting for transfers between devices, to_experts(): lax.all_to_all(shaped, 'fsdp', split_axis=0, concat_axis=0, tiled=True)  121 us
    unnamed x2, blocking collectives  110 us
  transfers between devices with their start and end apart: 17, of which 10 were waited for; matrix products, arithmetic and copies ran while one was open for 19% of the time, Pallas kernels for 0%

commit v1 on v0

--- a/solution.py
+++ b/solution.py
@@ -11,6 +11,28 @@
 EPSILON = 1e-06
 THETA = 1000000.0
 MASKED = -1e30
+
+
+def in_blocks(shard, dim, peers):
+    before, after = (shard.shape[:dim], shard.shape[dim + 1 :])
+    return jnp.moveaxis(shard.reshape(*before, peers, -1, *after), dim, 0)
+
+
+def joined_along(tiles, dim):
+    tiles = jnp.moveaxis(tiles, 0, dim)
+    dims = tiles.shape
+    return tiles.reshape(*dims[:dim], dims[dim] * dims[dim + 1], *dims[dim + 2 :])
+
+
+def exchange_directly(array, axis, split_dim, concat_dim):
+    size, place = (lax.axis_size(axis), lax.axis_index(axis))
+    tiles = in_blocks(array, split_dim, size)
+    outs = [tiles[place]]
+    for lap in range(1, size):
+        sent = tiles[(place + lap) % size]
+        outs.append(lax.ppermute(sent, axis, [(i, (i + lap) % size) for i in range(size)]))
+    tiles = jnp.stack(outs)[(place - jnp.arange(size)) % size]
+    return joined_along(tiles, concat_dim)
 
 
 def rms_forward(values, gain):
@@ -285,7 +307,7 @@
     grad_query_send = grad_query_blocks.reshape(seq_total, 1, heads_local, HD)
     grad_kv_send = jnp.stack([kv_grads[0], kv_grads[1]], axis=2).astype(jnp.bfloat16)
     grad_query_tok, grad_kv_tok = (
-        lax.all_to_all(grad_query_send, "seq", split_axis=0, concat_axis=1, tiled=True),
+        exchange_directly(grad_query_send, "seq", 0, 1),
         lax.all_to_all(grad_kv_send, "seq", split_axis=0, concat_axis=1, tiled=True),
     )
     grad_query_rot = grad_query_tok.reshape(tok_count, QH, HD).astype(jnp.float32)

time: 2950 us -> 2940 us (level)
    all_to_all x1, waiting for transfers between devices: 86.4 us -> 15 us  [per_device(): lax.all_to_all(grad_kv_send, 'seq', split_axis=0, concat_axis=1, tiled=True)]
    ppermute x0 -> x3, waiting for transfers between devices: none -> 49.2 us  [exchange_directly(): lax.ppermute(sent, axis, [(i, (i + lap) % size) for i in range(size)])]
    reduce_scatter x1, waiting for transfers between devices: 278 us -> 311 us  [per_device(): lax.psum_scatter(grad_out_local, ('seq', 'fsdp'), scatter_dimension=0, ti...]
    all_to_all x1 -> x0, blocking collectives: 30.9 us -> none  [per_device(): lax.all_to_all(grad_kv_send, 'seq', split_axis=0, concat_axis=1, tiled=True)]
  transfers between devices with their start and end apart: 17 -> 20, of which waited for: 10 -> 13; matrix products, arithmetic and copies ran while one was open for 19% -> 19% of each run, Pallas kernels for 0% -> 0%
where the time goes in v1:
time: 2940 us
  waiting for transfers between devices  1810 us (62%)
  blocking collectives  390 us (13%)
  matrix products  288 us (10%)
  local copies, waits for them, and re-layouts  224 us (8%)
  other arithmetic  164 us (6%)
  starting transfers between devices  41.6 us (1%)
    reduce_scatter x1, waiting for transfers between devices, per_device(): lax.psum_scatter(grad_qkv_local, ('seq', 'fsdp'), scatter_dimension=0, ti...  454 us
    reduce_scatter x1, waiting for transfers between devices, per_device(): lax.psum_scatter(grad_out_local, ('seq', 'fsdp'), scatter_dimension=0, ti...  311 us
    all_gather x1, waiting for transfers between devices, expert_weights(): lax.all_gather(w_gate_up, 'seq', axis=1, tiled=True)  290 us
    all_gather x1, waiting for transfers between devices, expert_weights(): lax.all_gather(w_down, 'seq', axis=2, tiled=True)  184 us
    all_gather x1, blocking collectives, per_device(): lax.all_gather(w_router, ('seq', 'fsdp'), axis=0, tiled=True)  146 us
    all_to_all x1, blocking collectives, from_experts(): lax.all_to_all(rows, 'fsdp', split_axis=0, concat_axis=0, tiled=True)  126 us
    all_to_all x2, waiting for transfers between devices, to_experts(): lax.all_to_all(shaped, 'fsdp', split_axis=0, concat_axis=0, tiled=True)  121 us
    unnamed x2, blocking collectives  118 us
  transfers between devices with their start and end apart: 20, of which 13 were waited for; matrix products, arithmetic and copies ran while one was open for 19% of the time, Pallas kernels for 0%

profile of v1, /device:TPU:1, one launch (start us, length us, event | category | flops | bytes accessed | tf_op | source)
XLA Modules:
  0.0 2935.1 jit_solution(5869002714759756999)
XLA Ops:
  10.9 43.2 %all-reduce = bf16[4352]{0:T(1024)(128)(2,1)S(1)} all-reduce(bf16[4352]{0:T(1024)(128)(2,1)S(1)} %dynamic-update-slice), channel_id=1, replica_groups=mesh['seq'=4,'fsdp'=8] {'seq','fsdp'}, use_global_device_ids=true, to_apply=%add | all-reduce | flops 4352 | bytes 17408
  55.0 93.7 %all-gather.6.cloned.1.call-done = bf16[2048,5120]{1,0:T(8,128)(2,1)} async-done(((bf16[64,5120]{1,0:T(8,128)(2,1)}), bf16[2048,5120]{1,0:T(8,128)(2,1)}) %all-gather.6.cloned.1.call-update) | async-done | bytes 20971536 | tf_op jit(solution)/shard_map/all_gather | solution.py:93
  193.0 87.3 %all-to-all-done = bf16[256,4,8,128]{0,3,2,1:T(8,128)(2,1)S(1)} async-done(((bf16[256,4,8,128]{0,3,2,1:T(8,128)(2,1)}), bf16[256,4,8,128]{0,3,2,1:T(8,128)(2,1)S(1)}, u32[]{:S(2)}, u32[]{:S(2)}) %all-to-all-start) | async-done | bytes 2097184 | tf_op jit(solution)/shard_map/all_to_all | solution.py:127
  286.4 33.8 %while.30 = (s32[]{:T(128)}, bf16[2,512,1,8,128]{4,3,1,0,2:T(8,128)(2,1)}, f32[2,1,8,512]{3,2,1,0:T(8,128)S(1)}, s32[2]{0:T(128)S(1)}, s32[]{:T(128)}, /*index=5...) while((s32[]{:T(128)}, ...), condition=%wide.region_6.7_spmd.clone.clone, body=%wide.region_3.6_spmd.clone.clone.sunk | while | flops 2199385600 | bytes 57285240 | solution.py:164
  339.1 99.5 %all-to-all-done.2 = bf16[1024,1,8,128]{3,2,1,0:T(8,128)(2,1)} async-done(((bf16[1024,1,8,128]{3,2,1,0:T(8,128)(2,1)}), bf16[1024,1,8,128]{3,2,1,0:T(8,128)(2,1)}, u32[]{:S(2)}, u32[]{:S(2)}) %all-to-all-start.2) | async-done | bytes 2097184 | tf_op jit(solution)/shard_map/all_to_all | solution.py:166
  480.0 290.5 %all-gather.10.cloned.1.call-done = bf16[4,2048,1536]{2,1,0:T(8,128)(2,1)} async-done(((bf16[4,512,1536]{2,1,0:T(8,128)(2,1)}), bf16[4,2048,1536]{2,1,0:T(8,128)(2,1)}) %all-gather.10.cloned.1.call-update) | async-done | bytes 25165840 | tf_op jit(solution)/shard_map/all_gather | solution.py:74
  770.5 25.7 fusion.75
  804.3 184.0 %all-gather.12.cloned.1.call-done = bf16[4,768,2048]{2,1,0:T(8,128)(2,1)} async-done(((bf16[4,768,512]{2,1,0:T(8,128)(2,1)}), bf16[4,768,2048]{2,1,0:T(8,128)(2,1)}) %all-gather.12.cloned.1.call-update) | async-done | bytes 12582928 | tf_op jit(solution)/shard_map/all_gather | solution.py:75
  988.3 16.0 convert_bitcast_fusion.2
  1021.0 145.7 %all-gather = bf16[32,64,32]{1,2,0:T(8,128)(2,1)S(1)} all-gather(bf16[1,64,32]{1,2,0:T(8,128)(2,1)S(1)} %bitcast.465), channel_id=1, replica_groups=mesh['seq'=4,'fsdp'=8] {'seq','fsdp'}, dimensions={0}, use_global_device_ids=true | all-gather | bytes 135168 | tf_op jit(solution)/shard_map/all_gather | solution.py:95
  1169.3 21.6 gather_fusion.3
  1201.4 24.6 gather_fusion.1
  1243.4 121.1 %all-to-all-done.5 = bf16[8,320,2048]{2,1,0:T(8,128)(2,1)} async-done(((bf16[8,320,2048]{2,1,0:T(8,128)(2,1)}), bf16[8,320,2048]{2,1,0:T(8,128)(2,1)}, u32[]{:S(2)}, u32[]{:S(2)}) %all-to-all-start.5) | async-done | bytes 10485792 | tf_op jit(solution)/shard_map/all_to_all | solution.py:64
  1364.5 16.6 bitcast_convert_fusion.1
  1381.6 16.3 convert_bitcast_fusion.4
  1408.5 27.1 bitcast_convert_fusion
  1435.8 23.6 convert_bitcast_fusion.1
  1469.5 125.7 %all_to_all.92 = bf16[8,320,2048]{2,1,0:T(8,128)(2,1)} all-to-all(bf16[8,320,2048]{2,1,0:T(8,128)(2,1)} %bitcast.435), channel_id=1, replica_groups=mesh['seq'=4,'fsdp'=8] {'fsdp'}, dimensions={0} | all-to-all | bytes 20971520 | tf_op jit(solution)/shard_map/all_to_all | solution.py:68
  1595.2 21.7 gather_fusion.4
  1616.9 17.4 convert_reduce_fusion
  1637.7 13.4 fusion.114
  1651.2 18.6 fusion.106
  1678.8 103.2 %all-to-all-done.7 = bf16[256,4,8,128]{3,2,0,1:T(8,128)(2,1)S(1)} async-done(((bf16[256,4,8,128]{3,2,0,1:T(8,128)(2,1)}), bf16[256,4,8,128]{3,2,0,1:T(8,128)(2,1)S(1)}, u32[]{:S(2)}, u32[]{:S(2)}) %all-to-all-start.7) | async-done | bytes 2097184 | tf_op jit(solution)/shard_map/all_to_all | solution.py:271
  1783.6 91.2 %while.31 = (s32[]{:T(128)}, f32[1024,1,128]{0,2,1:T(8,128)}, f32[1024,1,128]{0,2,1:T(8,128)}, bf16[2,512,1,8,128]{4,3,1,0,2:T(8,128)(2,1)}, bf16[2,512,1,8,128]...) while((s32[]{:T(128)}, f32[1024,1,128]{0,2,1:T(8,128)}, ...), condition=%wide.region_20.22_spmd.clone.clone, body=%wide.region_18.21_spmd.clone.clone.sunk | while | flops 5409207808 | bytes 199187792 | solution.py:304
  1791.9 11.0 fusion.198
  1904.0 35.0 %collective-permute-done.1 = bf16[256,1,8,128]{3,2,0,1:T(8,128)(2,1)} collective-permute-done((bf16[256,1,8,128]{3,2,0,1:T(8,128)(2,1)S(1)}, bf16[256,1,8,128]{3,2,0,1:T(8,128)(2,1)}, u32[]{:S(2)}, u32[]{:S(2)}) %collective-permute-start.1) | collective-permute-done | bytes 524320 | tf_op jit(solution)/shard_map/ppermute | solution.py:33
  1988.4 15.0 all-to-all-done.8
  2012.7 18.6 fusion.107
  2057.0 12.0 fusion.104
  2069.0 75.3 %all-reduce.1 = f32[4352]{0:T(1024)S(1)} all-reduce(f32[4352]{0:T(1024)S(1)} %pad_maximum_fusion.9), channel_id=5, replica_groups=mesh['seq'=4,'fsdp'=8] {'seq','fsdp'}, use_global_device_ids=true, to_apply=%region_31.33.clone | all-reduce | flops 4352 | bytes 34816
  2163.3 310.7 %reduce-scatter.10.cloned.1.call-done = f32[128,2048]{1,0:T(8,128)} async-done(((f32[4096,2048]{1,0:T(8,128)}), f32[128,2048]{1,0:T(8,128)}) %reduce-scatter.10.cloned.1.call-update) | async-done | bytes 1048592 | tf_op jit(solution)/shard_map/reduce_scatter | solution.py:344
  2474.0 454.2 %reduce-scatter.8.cloned.1.call-done = f32[64,5120]{1,0:T(8,128)} async-done(((f32[2048,5120]{1,0:T(8,128)}), f32[64,5120]{1,0:T(8,128)}) %reduce-scatter.8.cloned.1.call-update) | async-done | bytes 1310736 | tf_op jit(solution)/shard_map/reduce_scatter | solution.py:343
  (394 shorter events, 450.4 us)
Async XLA Ops:
  7.2 141.5 %all-gather.6.cloned.1.call-start = ((), (), s32[]{:S(2)}) async-start(), calls=%async_computation.14 | async-start | bytes 21626880 | tf_op jit(solution)/shard_map/all_gather | solution.py:93
  7.9 435.0 %all-gather.8.cloned.1.call-start = ((), (), s32[]{:S(2)}) async-start(), calls=%async_computation.15 | async-start | bytes 17301504 | tf_op jit(solution)/shard_map/all_gather | solution.py:94
  8.7 761.8 %all-gather.10.cloned.1.call-start = ((), (), s32[]{:S(2)}) async-start(), calls=%async_computation.16 | async-start | bytes 31457280 | tf_op jit(solution)/shard_map/all_gather | solution.py:74
  10.4 175.6 %copy-start.36 = (f32[256,64]{0,1:T(8,128)}, f32[256,64]{0,1:T(8,128)S(1)}, u32[]{:S(2)}) copy-start(f32[256,64]{0,1:T(8,128)S(1)} %get-tuple-element.498) | copy-start | bytes 196612
  10.5 151.6 %copy-start.32 = (f32[256,64]{1,0:T(8,128)}, f32[256,64]{1,0:T(8,128)S(1)}, u32[]{:S(2)}) copy-start(f32[256,64]{1,0:T(8,128)S(1)} %copy.364) | copy-start | bytes 196612
  54.4 94.3 %copy-start.58 = (f32[256]{0:T(256)}, f32[256]{0:T(256)S(1)}, u32[]{:S(2)}) copy-start(f32[256]{0:T(256)S(1)} %add_rsqrt_fusion.3) | copy-start | bytes 3076
  54.4 107.5 %copy-start.66 = (f32[128]{0:T(128)}, f32[128]{0:T(128)S(1)}, u32[]{:S(2)}) copy-start(f32[128]{0:T(128)S(1)} %get-tuple-element.494) | copy-start | bytes 1540
  54.4 128.7 %copy-start.68 = (f32[128]{0:T(128)}, f32[128]{0:T(128)S(1)}, u32[]{:S(2)}) copy-start(f32[128]{0:T(128)S(1)} %get-tuple-element.495) | copy-start | bytes 1540
  55.0 93.7 %copy-start.43 = (f32[2048]{0:T(1024)}, f32[2048]{0:T(1024)S(1)}, u32[]{:S(2)}) copy-start(f32[2048]{0:T(1024)S(1)} %get-tuple-element.493) | copy-start | bytes 24580
  163.4 24.8 all-to-all-start.1
  188.2 92.1 %all-to-all-start = ((bf16[256,4,8,128]{0,3,2,1:T(8,128)(2,1)}), bf16[256,4,8,128]{0,3,2,1:T(8,128)(2,1)S(1)}, u32[]{:S(2)}, u32[]{:S(2)}) async-start(bf16[256,4,8,128]{0,3,2,1:T(8,128)(2,1)} %pad_maximum_fusion.3), calls=%async_computation | async-start | bytes 4194304 | tf_op jit(solution)/shard_map/all_to_all | solution.py:127
  320.3 122.6 %copy-start.1 = (bf16[2,512,1,8,128]{4,1,3,2,0:T(8,128)(2,1)}, bf16[2,512,1,8,128]{4,1,3,2,0:T(8,128)(2,1)S(1)}, u32[]{:S(2)}) copy-start(bf16[2,512,1,8,128]{4,1,3,2,0:T(8,128)(2,1)S(1)} %get-tuple-element.706) | copy-start | bytes 6291460
  320.3 122.6 %copy-start.6 = (bf16[1024,1,128]{2,0,1:T(8,128)(2,1)}, bf16[1024,1,128]{2,0,1:T(8,128)(2,1)S(1)}, u32[]{:S(2)}) copy-start(bf16[1024,1,128]{2,0,1:T(8,128)(2,1)S(1)} %get-tuple-element.713) | copy-start | bytes 786436
  321.0 117.6 %all-to-all-start.2 = ((bf16[1024,1,8,128]{3,2,1,0:T(8,128)(2,1)}), bf16[1024,1,8,128]{3,2,1,0:T(8,128)(2,1)}, u32[]{:S(2)}, u32[]{:S(2)}) async-start(bf16[1024,1,8,128]{3,2,1,0:T(8,128)(2,1)} %bitcast.17), calls=%async_computation.2 | async-start | bytes 4194304 | tf_op jit(solution)/shard_map/all_to_all | solution.py:166
  325.5 117.4 %copy-start.12 = (bf16[1,256,2048]{2,1,0:T(8,128)(2,1)S(1)}, bf16[1,256,2048]{2,1,0:T(8,128)(2,1)}, u32[]{:S(2)}) copy-start(bf16[1,256,2048]{2,1,0:T(8,128)(2,1)} %param.17) | copy-start | bytes 3145732
  325.5 662.8 %all-gather.12.cloned.1.call-start = ((), (), s32[]{:S(2)}) async-start(), calls=%async_computation.17 | async-start | bytes 15728640 | tf_op jit(solution)/shard_map/all_gather | solution.py:75
  474.1 296.5 %all-to-all-start.3 = ((bf16[8,320,2048]{2,1,0:T(8,128)(2,1)}), bf16[8,320,2048]{2,1,0:T(8,128)(2,1)}, u32[]{:S(2)}, u32[]{:S(2)}) async-start(bf16[8,320,2048]{2,1,0:T(8,128)(2,1)} %broadcast_select_fusion.1), calls=%async_computation.3 | async-start | bytes 20971520 | tf_op jit(solution)/shard_map/all_to_all | solution.py:64
  1014.5 154.7 %all-to-all-start.4 = ((bf16[8,320,2048]{2,1,0:T(8,128)(2,1)}), bf16[8,320,2048]{2,1,0:T(8,128)(2,1)}, u32[]{:S(2)}, u32[]{:S(2)}) async-start(bf16[8,320,2048]{2,1,0:T(8,128)(2,1)} %bitcast.432), calls=%async_computation.4 | async-start | bytes 20971520 | tf_op jit(solution)/shard_map/all_to_all | solution.py:68
  1020.2 148.9 %copy-start.54 = (s32[1,256,8]{1,2,0:T(8,128)S(1)}, s32[1,256,8]{1,2,0:T(8,128)}, u32[]{:S(2)}) copy-start(s32[1,256,8]{1,2,0:T(8,128)} %param.20) | copy-start | bytes 24580
  1236.0 128.6 %all-to-all-start.5 = ((bf16[8,320,2048]{2,1,0:T(8,128)(2,1)}), bf16[8,320,2048]{2,1,0:T(8,128)(2,1)}, u32[]{:S(2)}, u32[]{:S(2)}) async-start(bf16[8,320,2048]{2,1,0:T(8,128)(2,1)} %broadcast_select_fusion), calls=%async_computation.5 | async-start | bytes 20971520 | tf_op jit(solution)/shard_map/all_to_all | solution.py:64
  1241.2 797.2 %reduce-scatter.16.cloned.1.call-start = ((), (), s32[]{:S(2)}) async-start(), calls=%async_computation.22 | async-start | bytes 1081344
  1243.4 905.0 %reduce-scatter.14.cloned.1.call-start = ((), (), s32[]{:S(2)}) async-start(), calls=%async_computation.21 | async-start | bytes 15728640 | tf_op jit(solution)/shard_map/reduce_scatter | solution.py:245
  1381.2 772.8 %reduce-scatter.12.cloned.1.call-start = ((), (), s32[]{:S(2)}) async-start(), calls=%async_computation.20 | async-start | bytes 31457280 | tf_op jit(solution)/shard_map/reduce_scatter | solution.py:242
  1435.6 1038.4 %reduce-scatter.10.cloned.1.call-start = ((), (), s32[]{:S(2)}) async-start(), calls=%async_computation.19 | async-start | bytes 34603008 | tf_op jit(solution)/shard_map/reduce_scatter | solution.py:344
  1469.5 125.7 %copy-start.52 = (s32[2048]{0:T(1024)S(1)}, s32[2048]{0:T(1024)}, u32[]{:S(2)}) copy-start(s32[2048]{0:T(1024)} %copy-done.51) | copy-start | bytes 24580
  1673.6 110.0 %copy-start.76 = (s32[2]{0:T(128)S(1)}, s32[2]{0:T(128)}, u32[]{:S(2)}) copy-start(s32[2]{0:T(128)} %copy-done.75) | copy-start | bytes 28
  1673.6 108.4 %all-to-all-start.7 = ((bf16[256,4,8,128]{3,2,0,1:T(8,128)(2,1)}), bf16[256,4,8,128]{3,2,0,1:T(8,128)(2,1)S(1)}, u32[]{:S(2)}, u32[]{:S(2)}) async-start(bf16[256,4,8,128]{3,2,0,1:T(8,128)(2,1)} %copy.384), calls=%async_computation.7 | async-start | bytes 4194304 | tf_op jit(solution)/shard_map/all_to_all | solution.py:271
  1877.4 26.6 collective-permute-start
  1877.4 61.6 %collective-permute-start.1 = (bf16[256,1,8,128]{3,2,0,1:T(8,128)(2,1)S(1)}, bf16[256,1,8,128]{3,2,0,1:T(8,128)(2,1)}, u32[]{:S(2)}, u32[]{:S(2)}) collective-permute-start(bf16[256,1,8,128]{3,2,0,1:T(8,128)(2,1)S(1)} %get-tuple-element.479), channel_id=1, source_target_pairs={{0,16},{8,24},{16,0},{24,8},{1,17},{9,25},{17,1},{25,9},{2,18},{10... | collective-permute-start | bytes 1572872 | tf_op jit(solution)/shard_map/ppermute | solution.py:33
  1877.4 67.7 %collective-permute-start.2 = (bf16[256,1,8,128]{3,2,0,1:T(8,128)(2,1)S(1)}, bf16[256,1,8,128]{3,2,0,1:T(8,128)(2,1)}, u32[]{:S(2)}, u32[]{:S(2)}) collective-permute-start(bf16[256,1,8,128]{3,2,0,1:T(8,128)(2,1)S(1)} %get-tuple-element.478), channel_id=1, source_target_pairs={{0,24},{8,0},{16,8},{24,16},{1,25},{9,1},{17,9},{25,17},{2,26},{10... | collective-permute-start | bytes 1572872 | tf_op jit(solution)/shard_map/ppermute | solution.py:33
  1891.7 111.7 %all-to-all-start.8 = ((bf16[1024,1,2,128]{3,2,1,0:T(2,128)(2,1)}), bf16[1024,1,2,128]{3,2,1,0:T(2,128)(2,1)}, u32[]{:S(2)}, u32[]{:S(2)}) async-start(bf16[1024,1,2,128]{3,2,1,0:T(2,128)(2,1)} %copy.396), calls=%async_computation.8 | async-start | bytes 1048576 | tf_op jit(solution)/shard_map/all_to_all | solution.py:311
  1895.8 1032.4 %reduce-scatter.8.cloned.1.call-start = ((), (), s32[]{:S(2)}) async-start(), calls=%async_computation.18 | async-start | bytes 43253760 | tf_op jit(solution)/shard_map/reduce_scatter | solution.py:343
  (71 other events, 660.1 us)
Sparse Core Ops, SparseCore 0:
  10.9 137.8 all-gather.5
  151.6 149.4 all-gather.7
  302.7 467.7 all-gather.9
  771.9 216.3 all-gather.11
  1243.9 132.2 reduce-scatter.15
  1381.3 211.4 reduce-scatter.13
  1595.2 506.0 reduce-scatter.11
  2104.1 369.8 reduce-scatter.9
  2476.9 451.2 reduce-scatter.7
